TPU v7x, 32 devices: a whole 2x2x4 slice. The times are simulated.
32 devices in a mesh: band: 16 (over z, y, core), chan: 2 (over x).
Axes of the slice: x: 2, y: 2, z: 4, core: 2. Of those that a mesh axis runs over, the one named last changes fastest.
Arguments:
- fine_features: bfloat16 [2, 192, 128, 512], P(None, 'chan', 'band'), may hold values from -100 to 100
- coarse_level: bfloat16 [2, 256, 64, 256], P(None, 'chan', 'band'), may hold values from -100 to 100
- lat_weight: bfloat16 [256, 192], P('chan'), may hold values from -0.4375 to 0.4375
- lat_gain: bfloat16 [256], P('chan'), may hold values from 0.099609375 to 1.8984375
- lat_shift: bfloat16 [256], P('chan'), may hold values from -3 to 3
- out_weight: bfloat16 [3, 3, 256, 256], P(None, None, 'chan'), may hold values from -0.125 to 0.125
- out_gain: bfloat16 [256], P('chan'), may hold values from 0.099609375 to 1.8984375
- out_shift: bfloat16 [256], P('chan'), may hold values from -3 to 3
- mask_weight: bfloat16 [256, 256], P('chan'), may hold values from -0.375 to 0.375
- mask_bias: bfloat16 [256], P('chan'), may hold values from -1.796875 to 1.796875
- queries: bfloat16 [200, 256], replicated, may hold values from -128 to 128
Outputs:
- log_probs: float32 [2, 200, 128, 512], P(None, None, ('band', 'chan'))
All inputs are finite; a program needn't handle non-finite values.
Results may differ from a plain program's by a relative error of at most 0.0058.
Values may be sent and summed in bfloat16 or wider, within the bound.
A program may use at most 128 MiB of HBM per device.

v0:
```python
import functools
import math

import jax
import jax.numpy as jnp
from jax import lax
from jax.experimental import pallas as pl
from jax.experimental.pallas import tpu as pltpu
from jax.sharding import PartitionSpec as P

D = 256
GROUPS = 32
EPS = 1e-05
MESH = pl.DeviceIdType.MESH
F32 = jnp.float32
BF16 = jnp.bfloat16


def wait_on(ref, sem):
    pltpu.make_async_copy(ref, ref, sem).wait()


def kernel(
    bands, chans, pixel_count,
    fine, coarse, lat_in, par_in, conv_in, mask_in, queries,
    out,
    feats, level, ebuf, pbuf, wbuf, mbuf, wide, lat, cols_up, stacked, conv, rows_out, stat1, stat2,
    f_send, f_recv, fh_send, fh_recv, c_send, c_recv, ch_send, ch_recv,
    e_send, e_recv, w_send, w_recv, q_send, q_recv, s_send, s_recv, o_sem,
):
    images, band_rows, in_ch, width = fine.shape
    rows = band_rows // chans
    c_rows = coarse.shape[1] // chans
    c_ch = coarse.shape[2]
    share = lat_in.shape[1]
    quad = math.gcd(bands, 4)
    quarter = share // quad
    gsize = D // GROUPS
    total = bands * chans
    b = lax.axis_index("band")
    c = lax.axis_index("chan")
    me = b * chans + c
    sends = []

    def send(src, dst, ssem, rsem, tb, tc, maybe_self):
        def remote():
            return pltpu.make_async_remote_copy(
                src_ref=src, dst_ref=dst, send_sem=ssem, recv_sem=rsem,
                device_id=(tb, tc), device_id_type=MESH,
            )

        if not maybe_self:
            remote().start()
            sends.append((remote, None))
            return
        is_self = jnp.logical_and(tb == b, tc == c)

        @pl.when(is_self)
        def _():
            pltpu.make_async_copy(src, dst, rsem).start()

        @pl.when(jnp.logical_not(is_self))
        def _():
            remote().start()

        sends.append((remote, is_self))

    def block(index, size):
        return pl.ds(pl.multiple_of(index * size, size), size)

    def gather(src, dst, ssem, rsem):
        pltpu.make_async_copy(src, dst.at[c], rsem.at[0]).start()
        for s in range(1, chans):
            t = lax.rem(c + s, chans)
            send(src, dst.at[c], ssem.at[s], rsem.at[s], b, t, False)

    spot = lax.rem(b, quad)

    def quarter_of(owner, part):
        return pl.ds(pl.multiple_of(owner * share + part * quarter, quarter), quarter)

    def weights_across(src, dst, ssem, rsem):
        pltpu.make_async_copy(src, dst.at[:, block(c, share)], rsem.at[0]).start()
        for s in range(1, chans):
            t = lax.rem(c + s, chans)
            send(
                src.at[:, pl.ds(pl.multiple_of(spot * quarter, quarter), quarter)],
                dst.at[:, quarter_of(c, spot)], ssem.at[s], rsem.at[s], b, t, False,
            )

    def weights_around(dst, rsem, ssem2, rsem2):
        for s in range(1, chans):
            wait_on(dst.at[:, pl.ds(0, quarter)], rsem.at[s])
            owner = lax.rem(c - s + chans, chans)
            piece = dst.at[:, quarter_of(owner, spot)]
            for m in range(1, quad):
                mate = b - spot + lax.rem(spot + m, quad)
                send(piece, piece, ssem2.at[s, m], rsem2.at[s, m], mate, c, False)

    def wait_weights(dst, rsem, rsem2):
        wait_on(dst.at[:, pl.ds(0, share)], rsem.at[0])
        for s in range(1, chans):
            for m in range(1, quad):
                wait_on(dst.at[:, pl.ds(0, quarter)], rsem2.at[s, m])

    def main_rows(src, dst, n, size, ch, ssem, rsem):
        for s in range(chans):
            t = lax.rem(c + s, chans)
            piece = src.at[n, pl.ds(t * size, size)]
            place = dst.at[n, pl.ds(1, size), block(c, ch)]
            if s == 0:
                pltpu.make_async_copy(piece, place, rsem.at[n, 0]).start()
            else:
                send(piece, place, ssem.at[n, s], rsem.at[n, s], b, t, False)

    def halo_rows(src, dst, n, size, ch, ssem, rsem):
        for s in range(chans):
            t = lax.rem(c + s, chans)
            k = (s + 1) % chans
            to = lax.rem(b * chans + t + 1, total)
            send(
                src.at[n, (t + 1) * size - 1], dst.at[n, 0, block(c, ch)],
                ssem.at[n, 0, s], rsem.at[n, 0, k], to // chans, lax.rem(to, chans), k == 0,
            )
            k = (s - 1) % chans
            to = lax.rem(b * chans + t - 1 + total, total)
            send(
                src.at[n, t * size], dst.at[n, size + 1, block(c, ch)],
                ssem.at[n, 1, s], rsem.at[n, 1, k], to // chans, lax.rem(to, chans), k == 0,
            )

    def wait_main(dst, n, size, ch, rsem):
        for s in range(chans):
            wait_on(dst.at[n, pl.ds(1, size), pl.ds(0, ch)], rsem.at[n, s])

    def wait_halo(dst, n, size, ch, rsem):
        for side in range(2):
            for s in range(chans):
                wait_on(dst.at[n, side * (size + 1), pl.ds(0, ch)], rsem.at[n, side, s])

    gather(lat_in, ebuf, e_send.at[0], e_recv.at[0])
    gather(par_in, pbuf, e_send.at[1], e_recv.at[1])
    for n in range(images):
        main_rows(fine, feats, n, rows, in_ch, f_send, f_recv)
    weights_across(conv_in, wbuf, w_send.at[0], w_recv.at[0])
    weights_across(mask_in, mbuf, w_send.at[1], w_recv.at[1])
    halo_rows(fine, feats, 0, rows, in_ch, fh_send, fh_recv)

    local_count = float(gsize * rows * width)
    lane = lax.broadcasted_iota(jnp.int32, (GROUPS, 128), 1)
    sub = lax.broadcasted_iota(jnp.int32, (GROUPS, 128), 0)

    def fold(x):
        acc = x[:, 0:128]
        for k in range(1, width // 128):
            acc = acc + x[:, k * 128:(k + 1) * 128]
        return acc

    def group_sum(x):
        x = jnp.sum(x.reshape(GROUPS, gsize, x.shape[1]), axis=1)
        return jnp.sum(x, axis=1, keepdims=True)

    def to_channels(col):
        return jnp.broadcast_to(col[:, None, :], (GROUPS, gsize, 1)).reshape(D, 1)

    def at_lanes(col, slot):
        return jnp.where(lane == sub + slot * GROUPS, jnp.broadcast_to(col, (GROUPS, 128)), 0.0)

    def from_lanes(row, slot):
        spread = jnp.where(lane == sub + slot * GROUPS, jnp.broadcast_to(row, (GROUPS, 128)), 0.0)
        return jnp.sum(spread, axis=1, keepdims=True)

    def produce(ref, n, first, compute):
        def step(r, acc):
            y = compute(r)
            ref[n, r + first] = y
            return acc + fold(y)

        s = group_sum(lax.fori_loop(0, rows, step, jnp.zeros((D, 128), F32)))
        mean = to_channels(s / local_count)

        def spread(r, acc):
            d = ref[n, r + first] - mean
            return acc + fold(d * d)

        m2 = group_sum(lax.fori_loop(0, rows, spread, jnp.zeros((D, 128), F32)))
        return at_lanes(s, n) + at_lanes(m2, images + n)

    def exchange(stats, buf, which):
        buf[0] = jnp.sum(stats, axis=0, keepdims=True)

        def one(k, carry):
            to = lax.rem(me + k, total)
            pltpu.make_async_remote_copy(
                src_ref=buf.at[0], dst_ref=buf.at[k],
                send_sem=s_send.at[which], recv_sem=s_recv.at[which],
                device_id=(to // chans, lax.rem(to, chans)), device_id_type=MESH,
            ).start()
            return carry

        lax.fori_loop(1, total, one, 0)

    def combined(buf, which):
        wait_on(buf.at[pl.ds(1, total - 1)], s_recv.at[which])
        parts = buf[...]
        sums = jnp.sum(parts, axis=0)
        mean = sums / pixel_count
        off = parts / local_count - mean[None]
        m2 = pltpu.roll(sums, 128 - images * GROUPS, 1)
        var = (m2 + local_count * jnp.sum(off * off, axis=0)) / pixel_count
        inv = lax.rsqrt(var + EPS)
        return [
            (to_channels(from_lanes(mean, n)), to_channels(from_lanes(inv, n)))
            for n in range(images)
        ]

    for k in range(2):
        for s in range(chans):
            wait_on((ebuf, pbuf)[k].at[0], e_recv.at[k, s])
    square = (
        lax.broadcasted_iota(jnp.int32, (share, share), 0)
        == lax.broadcasted_iota(jnp.int32, (share, share), 1)
    )

    def column(k):
        return jnp.concatenate([
            jnp.sum(jnp.where(
                square, jnp.broadcast_to(pbuf[s].astype(F32)[k:k + 1], (share, share)), 0.0,
            ), axis=1, keepdims=True)
            for s in range(chans)
        ], axis=0)

    lat_gain, lat_shift, out_gain, out_shift, bias = (column(k) for k in range(5))

    def lateral(features):
        return jnp.concatenate([
            lax.dot_general(
                ebuf[s], features, (((0,), (0,)), ((), ())), preferred_element_type=F32)
            for s in range(chans)
        ], axis=0)

    stats = jnp.zeros((GROUPS, 128), F32)
    for n in range(images):
        wait_main(feats, n, rows, in_ch, f_recv)
        stats = stats + produce(lat, n, 1, lambda r, n=n: lateral(feats[n, r + 1]))
    exchange(stats, stat1, 0)
    for n in range(images):
        if n > 0:
            halo_rows(fine, feats, n, rows, in_ch, fh_send, fh_recv)
        main_rows(coarse, level, n, c_rows, c_ch, c_send, c_recv)
        halo_rows(coarse, level, n, c_rows, c_ch, ch_send, ch_recv)
    weights_around(wbuf, w_recv.at[0], q_send.at[0], q_recv.at[0])
    weights_around(mbuf, w_recv.at[1], q_send.at[1], q_recv.at[1])

    src_col = lax.broadcasted_iota(jnp.int32, (width // 2, width), 0)
    dst_col = lax.broadcasted_iota(jnp.int32, (width // 2, width), 1)
    half = dst_col // 2
    near = jnp.where(src_col == half, 0.75, 0.0)
    other = jnp.clip(jnp.where(dst_col - 2 * half == 0, half - 1, half + 1), 0, width // 2 - 1)
    up = (near + jnp.where(src_col == other, 0.25, 0.0)).astype(BF16)
    lane_w = lax.broadcasted_iota(jnp.int32, (D, width), 1)

    stats = jnp.zeros((GROUPS, 128), F32)
    norms = None
    for n in range(images):
        wait_halo(feats, n, rows, in_ch, fh_recv)
        for j in (0, rows + 1):
            lat[n, j] = lateral(feats[n, j])
        wait_main(level, n, c_rows, c_ch, c_recv)
        wait_halo(level, n, c_rows, c_ch, ch_recv)

        def widen(k, carry):
            cols_up[k] = jnp.dot(level[n, k], up, preferred_element_type=F32)
            return carry

        lax.fori_loop(0, c_rows + 2, widen, 0)

        @pl.when(me == 0)
        def _():
            cols_up[0] = cols_up[1]

        @pl.when(me == total - 1)
        def _():
            cols_up[c_rows + 1] = cols_up[c_rows]

        if norms is None:
            norms = combined(stat1, 0)
        mean, inv = norms[n]
        scale = inv * lat_gain

        def join(j, carry):
            k = j // 2
            even = j - 2 * k == 0
            w0 = jnp.where(even, 0.75, 0.25)
            w1 = jnp.where(even, 0.25, 0.75)
            upsampled = w0 * cols_up[k] + w1 * cols_up[k + 1]
            joined = (lat[n, j] - mean) * scale + lat_shift + upsampled
            inside = jnp.logical_and(me * rows + j >= 1, me * rows + j <= total * rows)
            joined = jnp.where(inside, joined, 0.0)
            left = jnp.where(lane_w == 0, 0.0, pltpu.roll(joined, 1, 1))
            right = jnp.where(lane_w == width - 1, 0.0, pltpu.roll(joined, width - 1, 1))
            base = pl.multiple_of(j * 3 * D, D)
            stacked[pl.ds(base, D)] = left.astype(BF16)
            stacked[pl.ds(base + D, D)] = joined.astype(BF16)
            stacked[pl.ds(base + 2 * D, D)] = right.astype(BF16)
            return carry

        lax.fori_loop(0, rows + 2, join, 0)
        if n == 0:
            wait_weights(wbuf, w_recv.at[0], q_recv.at[0])
            for k in range(9):
                wide[:, k * D:(k + 1) * D] = wbuf[k]

        def convolve(r):
            base = pl.multiple_of(r * 3 * D, D)
            return jnp.dot(wide[...], stacked[pl.ds(base, 9 * D)], preferred_element_type=F32)

        stats = stats + produce(conv, n, 0, convolve)

    exchange(stats, stat2, 1)
    wait_weights(mbuf, w_recv.at[1], q_recv.at[1])
    norms = combined(stat2, 1)
    for n in range(images):
        mean, inv = norms[n]
        scale = inv * out_gain

        def finish(r, carry):
            act = jnp.maximum((conv[n, r] - mean) * scale + out_shift, 0.0).astype(BF16)
            mixed = jnp.dot(mbuf[0], act, preferred_element_type=F32)
            features = (mixed + bias).astype(BF16)
            logits = jnp.dot(queries[...], features, preferred_element_type=F32)
            shifted = logits - jnp.max(logits, axis=0, keepdims=True)
            norm = jnp.log(jnp.sum(jnp.exp(shifted), axis=0, keepdims=True))
            rows_out[n, r] = shifted - norm
            pltpu.make_async_copy(rows_out.at[n, r], out.at[n, r], o_sem.at[n, r]).start()
            return carry

        lax.fori_loop(0, rows, finish, 0)

    for n in range(images):
        for r in range(rows):
            pltpu.make_async_copy(rows_out.at[n, r], out.at[n, r], o_sem.at[n, r]).wait()
    for which, buf in ((0, stat1), (1, stat2)):
        wait_on(buf.at[pl.ds(1, total - 1)], s_send.at[which])
    for remote, is_self in sends:
        if is_self is None:
            remote().wait_send()
        else:
            @pl.when(jnp.logical_not(is_self))
            def _():
                remote().wait_send()


def per_device(
    bands, chans,
    fine_features, coarse_level, lat_weight, lat_gain, lat_shift, out_weight, out_gain, out_shift,
    mask_weight, mask_bias, queries,
):
    images, in_ch, band_rows, width = fine_features.shape
    share = lat_weight.shape[0]
    c_ch, c_band = coarse_level.shape[1], coarse_level.shape[2]
    rows, c_rows = band_rows // chans, c_band // chans
    query_count = queries.shape[0]
    pixel_count = float(D // GROUPS * band_rows * bands * width)
    fine = jnp.transpose(fine_features, (0, 2, 1, 3))
    coarse = jnp.transpose(coarse_level, (0, 2, 1, 3))
    params = jnp.stack([lat_gain, lat_shift, out_gain, out_shift, mask_bias], axis=0)
    params = jnp.pad(params, ((0, 16 - params.shape[0]), (0, 0)))
    anywhere = pl.BlockSpec(memory_space=pl.ANY)
    vmem = pl.BlockSpec(memory_space=pltpu.VMEM)
    dma = pltpu.SemaphoreType.DMA
    result = pl.pallas_call(
        functools.partial(kernel, bands, chans, pixel_count),
        out_shape=jax.ShapeDtypeStruct((images, rows, query_count, width), F32),
        in_specs=[anywhere] * 6 + [vmem],
        out_specs=anywhere,
        scratch_shapes=[
            pltpu.VMEM((images, rows + 2, chans * in_ch, width), BF16),
            pltpu.VMEM((images, c_rows + 2, chans * c_ch, width // 2), BF16),
            pltpu.VMEM((chans, chans * in_ch, share), BF16),
            pltpu.VMEM((chans, 16, share), BF16),
            pltpu.VMEM((9, D, D), BF16),
            pltpu.VMEM((1, D, D), BF16),
            pltpu.VMEM((D, 9 * D), BF16),
            pltpu.VMEM((images, rows + 2, D, width), F32),
            pltpu.VMEM((c_rows + 2, D, width), F32),
            pltpu.VMEM(((rows + 2) * 3 * D, width), BF16),
            pltpu.VMEM((images, rows, D, width), F32),
            pltpu.VMEM((images, rows, query_count, width), F32),
            pltpu.VMEM((bands * chans, 1, 128), F32),
            pltpu.VMEM((bands * chans, 1, 128), F32),
            dma((images, chans)), dma((images, chans)),
            dma((images, 2, chans)), dma((images, 2, chans)),
            dma((images, chans)), dma((images, chans)),
            dma((images, 2, chans)), dma((images, 2, chans)),
            dma((2, chans)), dma((2, chans)), dma((2, chans)), dma((2, chans)),
            dma((2, chans, 4)), dma((2, chans, 4)),
            dma((2,)), dma((2,)),
            dma((images, rows)),
        ],
        compiler_params=pltpu.CompilerParams(
            has_side_effects=True, vmem_limit_bytes=60 * 1024 * 1024),
    )(
        fine, coarse, lat_weight.T, params, out_weight.reshape(9, share, D), mask_weight[None],
        queries,
    )
    return jnp.transpose(result, (0, 2, 1, 3))


def solution(mesh):
    return jax.shard_map(
        functools.partial(per_device, mesh.shape["band"], mesh.shape["chan"]),
        mesh=mesh,
        in_specs=(
            P(None, "chan", "band", None),
            P(None, "chan", "band", None),
            P("chan", None),
            P("chan"),
            P("chan"),
            P(None, None, "chan", None),
            P("chan"),
            P("chan"),
            P("chan", None),
            P("chan"),
            P(),
        ),
        out_specs=P(None, None, ("band", "chan"), None),
        check_vma=False,
    )
```

profile of v0, /device:TPU:0, one launch (start us, length us, event | category | flops | bytes accessed | tf_op | source)
XLA Modules:
  0.0 86.7 jit_solution(11345100425485186588)
XLA Ops:
  0.0 0.7 stack.23
  0.7 0.6 pad.4.par_in
  1.3 1.9 %copy.18 = bf16[2,128,4,256]{3,1,2,0:T(8,128)(2,1)} copy(bf16[2,128,4,256]{3,2,1,0:T(4,128)(2,1)} %param.12) | data formatting | bytes 1048576 | tf_op args[1]
  3.2 3.0 %copy.17 = bf16[2,96,8,512]{3,1,2,0:T(8,128)(2,1)} copy(bf16[2,96,8,512]{3,2,1,0:T(8,128)(2,1)} %param.11) | data formatting | bytes 3145728 | tf_op args[0]
  6.3 74.6 %shard_map.109 = f32[2,4,200,512]{3,2,1,0:T(8,128)} custom-call(bf16[2,8,96,512]{3,2,1,0:T(8,128)(2,1)} %bitcast.16, bf16[2,4,128,256]{3,2,1,0:T(8,128)(2,1)} %bitcast.17, bf16[192,128]{1,0:T(8,128)(2,1)} %bitcast.20, bf16[16,128]{1,0:T(8,128)(2,1)} %pad.4.par_in, bf16[9,128,256]{2,1,0:T(8,128)(2,1)} %bitcast.18, bf16[1,128,256]{2,1,0:T(8,128)(2,1)} %bitcast.19, ...), custom_call_target="tpu_custom_call" | custom-call | tf_op jit(solution)/shard_map/pallas_call | solution.py:372
  80.9 5.7 %copy.14 = f32[2,200,4,512]{3,2,1,0:T(4,128)} copy(f32[2,200,4,512]{3,1,2,0:T(8,128)} %bitcast.15) | data formatting | bytes 6553600 | tf_op jit(solution)/shard_map/transpose | solution.py:407
where the time goes:
time: 86.9 us; the launch traced here: 86.7 us
  Pallas kernels  74.6 us (86%)
  local copies, waits for them, and re-layouts  12 us (14%)
    pallas_call x1, Pallas kernels, per_device(): pl.pallas_call(functools.partial(kernel, bands, chans, pixel_count), out_...  74.6 us
    transpose x1, local copies, waits for them, and re-layouts, per_device(): return jnp.transpose(result, (0, 2, 1, 3))  5.74 us
    unnamed x2, local copies, waits for them, and re-layouts  4.94 us

commit v1 on v0

v1 whole, which is shorter than its diff:
```python
import functools
import math

import jax
import jax.numpy as jnp
from jax import lax
from jax.experimental import pallas as pl
from jax.experimental.pallas import tpu as pltpu
from jax.sharding import PartitionSpec as P

D = 256
GROUPS = 32
EPS = 1e-05
LANES = 128
MESH = pl.DeviceIdType.MESH
F32 = jnp.float32
BF16 = jnp.bfloat16


def wait_on(ref, sem):
    pltpu.make_async_copy(ref, ref, sem).wait()


def across(x, times):
    return jnp.concatenate([x] * times, axis=1)


def log_softmax_row(centred, scale, offset, mask, bias, queries):
    act = jnp.maximum(centred * scale + offset, 0.0).astype(BF16)
    mixed = jnp.dot(mask, act, preferred_element_type=F32)
    features = (mixed + bias).astype(BF16)
    logits = jnp.dot(queries, features, preferred_element_type=F32)
    shifted = logits - jnp.max(logits, axis=0, keepdims=True)
    norm = jnp.log(jnp.sum(jnp.exp(shifted), axis=0, keepdims=True))
    return shifted - norm


def kernel(
    bands, chans, pixel_count,
    fine, coarse, lat_in, par0, par1, par2, par3, par4, conv_in, mask_in, queries,
    done, last_conv, last_coef, mask_out,
    raw, craw, tmp, ctmp, fsend, csend,
    feats, level, ebuf, pbuf, wbuf, mbuf, wlat, wide, lat, cols_up, stacked, conv, rows_out,
    coef, stat1, stat2,
    r_sem, f_send, f_recv, fh_send, fh_recv, c_send, c_recv, ch_send, ch_recv,
    e_send, e_recv, w_send, w_recv, q_send, q_recv, s_send, s_recv, o_sem, k_sem,
):
    images, in_ch, band_rows, width = fine.shape
    c_ch, c_band = coarse.shape[1], coarse.shape[2]
    rows, c_rows = band_rows // chans, c_band // chans
    half_w = width // 2
    share = lat_in.shape[1]
    quad = math.gcd(bands, 4)
    quarter = share // quad
    gsize = D // GROUPS
    total = bands * chans
    times = width // LANES
    last = images - 1
    b = lax.axis_index("band")
    c = lax.axis_index("chan")
    me = b * chans + c
    sends = []

    barrier = pltpu.get_barrier_semaphore()

    def greet(k, carry):
        to = lax.rem(me + k, total)
        pl.semaphore_signal(
            barrier, inc=1, device_id=(to // chans, lax.rem(to, chans)), device_id_type=MESH)
        return carry

    lax.fori_loop(1, total, greet, 0)
    for n in range(images):
        pltpu.make_async_copy(fine.at[n], raw.at[n], r_sem.at[0, n]).start()
        pltpu.make_async_copy(coarse.at[n], craw.at[n], r_sem.at[1, n]).start()

    def send(src, dst, ssem, rsem, tb, tc, only=None):
        def remote():
            return pltpu.make_async_remote_copy(
                src_ref=src, dst_ref=dst, send_sem=ssem, recv_sem=rsem,
                device_id=(tb, tc), device_id_type=MESH,
            )

        if only is None:
            remote().start()
        else:
            @pl.when(only)
            def _():
                remote().start()
        sends.append((remote, only))

    def block(index, size):
        return pl.ds(pl.multiple_of(index * size, size), size)

    def gather(src, dst, ssem, rsem):
        pltpu.make_async_copy(src, dst.at[c], rsem.at[0]).start()
        for s in range(1, chans):
            send(src, dst.at[c], ssem.at[s], rsem.at[s], b, lax.rem(c + s, chans))

    spot = lax.rem(b, quad)

    def quarter_of(owner, part):
        return pl.ds(pl.multiple_of(owner * share + part * quarter, quarter), quarter)

    def weights_across(src, dst, ssem, rsem):
        for s in range(1, chans):
            send(
                src.at[:, pl.ds(pl.multiple_of(spot * quarter, quarter), quarter)],
                dst.at[:, quarter_of(c, spot)], ssem.at[s], rsem.at[s], b, lax.rem(c + s, chans),
            )
        pltpu.make_async_copy(src, dst.at[:, block(c, share)], rsem.at[0]).start()

    def weights_around(dst, rsem, ssem2, rsem2):
        for s in range(1, chans):
            wait_on(dst.at[:, pl.ds(0, quarter)], rsem.at[s])
            owner = lax.rem(c - s + chans, chans)
            piece = dst.at[:, quarter_of(owner, spot)]
            for m in range(1, quad):
                mate = b - spot + lax.rem(spot + m, quad)
                send(piece, piece, ssem2.at[s, m], rsem2.at[s, m], mate, c)

    def wait_weights(dst, rsem, rsem2):
        wait_on(dst.at[:, pl.ds(0, share)], rsem.at[0])
        for s in range(1, chans):
            for m in range(1, quad):
                wait_on(dst.at[:, pl.ds(0, quarter)], rsem2.at[s, m])

    def main_rows(src, dst, n, size, ch, ssem, rsem):
        for s in range(1, chans):
            t = lax.rem(c + s, chans)
            send(
                src.at[n, pl.ds(t * size, size)], dst.at[n, pl.ds(1, size), block(c, ch)],
                ssem.at[n, s], rsem.at[n, s], b, t,
            )

    def halo_rows(src, dst, n, size, ch, ssem, rsem):
        for s in range(chans):
            t = lax.rem(c + s, chans)
            k = (s + 1) % chans
            to = lax.rem(b * chans + t + 1, total)
            send(
                src.at[n, (t + 1) * size - 1], dst.at[n, 0, block(c, ch)],
                ssem.at[n, 0, s], rsem.at[n, 0, k], to // chans, lax.rem(to, chans),
                c == 0 if k == 0 else None,
            )
            k = (s - 1) % chans
            to = lax.rem(b * chans + t - 1 + total, total)
            send(
                src.at[n, t * size], dst.at[n, size + 1, block(c, ch)],
                ssem.at[n, 1, s], rsem.at[n, 1, k], to // chans, lax.rem(to, chans),
                c == chans - 1 if k == 0 else None,
            )

    def keep_own(src, dst, n, size, ch):
        own = block(c, ch)
        for i in range(size):
            dst[n, i + 1, own] = src[n, c * size + i]

        @pl.when(c > 0)
        def _():
            dst[n, 0, own] = src[n, c * size - 1]

        @pl.when(c < chans - 1)
        def _():
            dst[n, size + 1, own] = src[n, (c + 1) * size]

    def wait_main(dst, n, size, ch, rsem):
        for s in range(1, chans):
            wait_on(dst.at[n, pl.ds(1, size), pl.ds(0, ch)], rsem.at[n, s])

    def wait_halo(dst, n, size, ch, rsem):
        for side in range(2):
            for s in range(chans):
                def arrive():
                    wait_on(dst.at[n, side * (size + 1), pl.ds(0, ch)], rsem.at[n, side, s])

                if s == 0:
                    pl.when(c == (0, chans - 1)[side])(arrive)
                else:
                    arrive()

    def by_rows(src, dst, buf, n, pitch):
        channels, height, columns = src.shape[1], src.shape[2], src.shape[3]

        def lanes(k, carry):
            col = pl.ds(pl.multiple_of(k * LANES, LANES), LANES)
            for ch in range(channels):
                buf[pl.ds(ch * pitch, height), :] = src[n, ch, :, col].astype(F32)
            for r in range(height):
                dst[n, r, :, col] = buf[pl.ds(r, channels, stride=pitch), :].astype(BF16)
            return carry

        lax.fori_loop(0, columns // LANES, lanes, 0)

    def fine_rows(n):
        pltpu.make_async_copy(fine.at[n], raw.at[n], r_sem.at[0, n]).wait()
        by_rows(raw, fsend, tmp, n, tmp.shape[0] // in_ch)

    def coarse_rows(n):
        pltpu.make_async_copy(coarse.at[n], craw.at[n], r_sem.at[1, n]).wait()
        by_rows(craw, csend, ctmp, n, ctmp.shape[0] // c_ch)

    fine_rows(0)
    pl.semaphore_wait(barrier, total - 1)
    gather(lat_in, ebuf, e_send.at[0], e_recv.at[0])
    for k, par in enumerate((par0, par1, par2, par3, par4)):
        gather(par, pbuf.at[k], e_send.at[k + 1], e_recv.at[k + 1])
    for n in range(images):
        if n > 0:
            fine_rows(n)
        main_rows(fsend, feats, n, rows, in_ch, f_send, f_recv)
    weights_across(conv_in, wbuf, w_send.at[0], w_recv.at[0])
    for n in range(images):
        coarse_rows(n)
        halo_rows(fsend, feats, n, rows, in_ch, fh_send, fh_recv)
        main_rows(csend, level, n, c_rows, c_ch, c_send, c_recv)
        halo_rows(csend, level, n, c_rows, c_ch, ch_send, ch_recv)
        if n == 0:
            weights_across(mask_in, mbuf, w_send.at[1], w_recv.at[1])
    for n in range(images):
        keep_own(fsend, feats, n, rows, in_ch)
        keep_own(csend, level, n, c_rows, c_ch)

    local_count = float(gsize * rows * width)
    lane = lax.broadcasted_iota(jnp.int32, (D, LANES), 1)
    group = lax.broadcasted_iota(jnp.int32, (D, LANES), 0) // gsize

    def fold(x):
        acc = x[:, 0:LANES]
        for k in range(1, times):
            acc = acc + x[:, k * LANES:(k + 1) * LANES]
        return acc

    def to_row(x, slot):
        s = jnp.sum(x, axis=1, keepdims=True)
        return jnp.sum(jnp.where(lane == group + slot * GROUPS, s, 0.0), axis=0, keepdims=True)

    def from_row(row, slot):
        spread = jnp.where(lane == group + slot * GROUPS, row, 0.0)
        return jnp.sum(spread, axis=1, keepdims=True)

    def first_shift(y):
        mean = from_row(to_row(fold(y), 0), 0) / float(gsize * width)
        return jnp.broadcast_to(mean, (D, LANES))

    def stat_rows(s1, s2, shift, slot, slots):
        a = to_row(s1, slot)
        m2 = to_row(s2, slot) - a * a / local_count
        here = lax.broadcasted_iota(jnp.int32, (1, LANES), 1) // GROUPS == slot
        m2 = jnp.where(here, m2, 0.0)
        own = jnp.sum(
            jnp.where(lane == group + slot * GROUPS, shift, 0.0), axis=0, keepdims=True)
        s = a + own * (local_count / gsize)
        return s + pltpu.roll(m2, slots * GROUPS, 1)

    def exchange(row, buf, which):
        buf[0] = row

        def one(k, carry):
            to = lax.rem(me + k, total)
            pltpu.make_async_remote_copy(
                src_ref=buf.at[0], dst_ref=buf.at[k],
                send_sem=s_send.at[which], recv_sem=s_recv.at[which],
                device_id=(to // chans, lax.rem(to, chans)), device_id_type=MESH,
            ).start()
            return carry

        lax.fori_loop(1, total, one, 0)

    def combined(buf, which, slots):
        wait_on(buf.at[pl.ds(1, total - 1)], s_recv.at[which])
        parts = buf[...]
        sums = jnp.sum(parts, axis=0)
        mean = sums / pixel_count
        off = parts / local_count - mean[None]
        m2 = pltpu.roll(sums, LANES - slots * GROUPS, 1)
        var = (m2 + local_count * jnp.sum(off * off, axis=0)) / pixel_count
        inv = lax.rsqrt(var + EPS)
        return [(from_row(mean, n), from_row(inv, n)) for n in range(slots)]

    for k in range(6):
        for s in range(chans):
            wait_on((pbuf.at[k - 1] if k else ebuf).at[0], e_recv.at[k, s])
    square = (
        lax.broadcasted_iota(jnp.int32, (share, share), 0)
        == lax.broadcasted_iota(jnp.int32, (share, share), 1)
    )

    def column(k):
        return jnp.concatenate([
            jnp.sum(jnp.where(
                square, jnp.broadcast_to(pbuf[k, s].astype(F32), (share, share)), 0.0,
            ), axis=1, keepdims=True)
            for s in range(chans)
        ], axis=0)

    lat_gain, lat_shift, out_gain, out_shift, bias = (column(k) for k in range(5))
    for s in range(chans):
        wlat[s * share:(s + 1) * share, :] = ebuf[s].astype(F32).T.astype(BF16)

    def lateral(features):
        return jnp.dot(wlat[...], features, preferred_element_type=F32)

    SHIFT, SCALE, OFFSET, S1, S2 = range(5)

    def centre_first(y, slot):
        coef[slot, SHIFT] = first_shift(y)
        coef[slot, S1] = jnp.zeros((D, LANES), F32)
        coef[slot, S2] = jnp.zeros((D, LANES), F32)

    def centre(y, slot):
        d = y - across(coef[slot, SHIFT], times)
        coef[slot, S1] = coef[slot, S1] + fold(d)
        coef[slot, S2] = coef[slot, S2] + fold(d * d)
        return d

    def set_norm(slot, mean, inv, gain, shift):
        scale = inv * gain
        coef[slot, SCALE] = jnp.broadcast_to(scale, (D, LANES))
        centred = jnp.broadcast_to(mean, (D, LANES)) - coef[slot, SHIFT]
        coef[slot, OFFSET] = shift - centred * scale

    row1 = jnp.zeros((1, LANES), F32)
    for n in range(images):
        wait_main(feats, n, rows, in_ch, f_recv)
        y = lateral(feats[n, 1])
        centre_first(y, n)
        lat[n, 1] = centre(y, n)

        def step(r, carry, n=n):
            lat[n, r + 1] = centre(lateral(feats[n, r + 1]), n)
            return carry

        lax.fori_loop(1, rows, step, 0)
        row1 = row1 + stat_rows(coef[n, S1], coef[n, S2], coef[n, SHIFT], n, images)
    exchange(row1, stat1, 0)
    weights_around(wbuf, w_recv.at[0], q_send.at[0], q_recv.at[0])

    src_col = lax.broadcasted_iota(jnp.int32, (half_w, width), 0)
    dst_col = lax.broadcasted_iota(jnp.int32, (half_w, width), 1)
    half = dst_col // 2
    near = jnp.where(src_col == half, 0.75, 0.0)
    other = jnp.clip(jnp.where(dst_col - 2 * half == 0, half - 1, half + 1), 0, half_w - 1)
    up = (near + jnp.where(src_col == other, 0.25, 0.0)).astype(BF16)
    lane_w = lax.broadcasted_iota(jnp.int32, (D, width), 1)

    for n in range(images):
        wait_halo(feats, n, rows, in_ch, fh_recv)
        for j in (0, rows + 1):
            lat[n, j] = lateral(feats[n, j]) - across(coef[n, SHIFT], times)
        if n == 0:
            norms = combined(stat1, 0, images)
            for m in range(images):
                set_norm(m, norms[m][0], norms[m][1], lat_gain, lat_shift)
        wait_main(level, n, c_rows, c_ch, c_recv)
        wait_halo(level, n, c_rows, c_ch, ch_recv)

        def widen(k, carry, n=n):
            cols_up[k] = jnp.dot(level[n, k], up, preferred_element_type=F32)
            return carry

        lax.fori_loop(0, c_rows + 2, widen, 0)

        @pl.when(me == 0)
        def _():
            cols_up[0] = cols_up[1]

        @pl.when(me == total - 1)
        def _():
            cols_up[c_rows + 1] = cols_up[c_rows]

        def join(j, carry, n=n):
            k = j // 2
            even = j - 2 * k == 0
            w0 = jnp.where(even, 0.75, 0.25)
            w1 = jnp.where(even, 0.25, 0.75)
            upsampled = w0 * cols_up[k] + w1 * cols_up[k + 1]
            joined = (
                lat[n, j] * across(coef[n, SCALE], times)
                + across(coef[n, OFFSET], times) + upsampled)
            inside = jnp.logical_and(me * rows + j >= 1, me * rows + j <= total * rows)
            joined = jnp.where(inside, joined, 0.0)
            left = jnp.where(lane_w == 0, 0.0, pltpu.roll(joined, 1, 1))
            right = jnp.where(lane_w == width - 1, 0.0, pltpu.roll(joined, width - 1, 1))
            base = pl.multiple_of(j * 3 * D, D)
            stacked[pl.ds(base, D)] = left.astype(BF16)
            stacked[pl.ds(base + D, D)] = joined.astype(BF16)
            stacked[pl.ds(base + 2 * D, D)] = right.astype(BF16)
            return carry

        lax.fori_loop(0, rows + 2, join, 0)
        if n == 0:
            wait_weights(wbuf, w_recv.at[0], q_recv.at[0])
            for k in range(9):
                wide[:, k * D:(k + 1) * D] = wbuf[k]

        def convolve(r):
            base = pl.multiple_of(r * 3 * D, D)
            return jnp.dot(wide[...], stacked[pl.ds(base, 9 * D)], preferred_element_type=F32)

        slot = images + n

        def keep(r, y, n=n, slot=slot):
            conv[n, r] = centre(y, slot)
            if n == last:
                pltpu.make_async_copy(conv.at[n, r], last_conv.at[r], k_sem.at[r]).start()

        y = convolve(0)
        centre_first(y, slot)
        keep(0, y)

        def more(r, carry):
            keep(r, convolve(r))
            return carry

        lax.fori_loop(1, rows, more, 0)
        exchange(
            stat_rows(coef[slot, S1], coef[slot, S2], coef[slot, SHIFT], 0, 1), stat2.at[n], 1 + n)
        if n == 0:
            weights_around(mbuf, w_recv.at[1], q_send.at[1], q_recv.at[1])

    wait_weights(mbuf, w_recv.at[1], q_recv.at[1])
    pltpu.make_async_copy(mbuf.at[0], mask_out, k_sem.at[rows]).start()
    for n in range(last):
        slot = images + n
        mean, inv = combined(stat2.at[n], 1 + n, 1)[0]
        set_norm(slot, mean, inv, out_gain, out_shift)

        def finish(r, carry, n=n, slot=slot):
            rows_out[n, r] = log_softmax_row(
                conv[n, r], across(coef[slot, SCALE], times), across(coef[slot, OFFSET], times),
                mbuf[0], bias, queries[...])
            pltpu.make_async_copy(rows_out.at[n, r], done.at[n, :, r], o_sem.at[n, r]).start()
            return carry

        lax.fori_loop(0, rows, finish, 0)

    slot = images + last
    mean, inv = combined(stat2.at[last], 1 + last, 1)[0]
    set_norm(slot, mean, inv, out_gain, out_shift)
    coef[slot, SHIFT] = jnp.broadcast_to(bias, (D, LANES))
    pltpu.make_async_copy(
        coef.at[slot, pl.ds(0, 3)], last_coef, k_sem.at[rows + 1]).start()

    for which in range(1 + images):
        buf = stat1 if which == 0 else stat2.at[which - 1]
        wait_on(buf.at[pl.ds(1, total - 1)], s_send.at[which])
    for remote, only in sends:
        if only is None:
            remote().wait_send()
        else:
            @pl.when(only)
            def _():
                remote().wait_send()
    for n in range(last):
        for r in range(rows):
            pltpu.make_async_copy(rows_out.at[n, r], done.at[n, :, r], o_sem.at[n, r]).wait()
    for r in range(rows):
        pltpu.make_async_copy(conv.at[last, r], last_conv.at[r], k_sem.at[r]).wait()
    pltpu.make_async_copy(mbuf.at[0], mask_out, k_sem.at[rows]).wait()
    pltpu.make_async_copy(coef.at[slot, pl.ds(0, 3)], last_coef, k_sem.at[rows + 1]).wait()


def tail(
    done, conv, coef_in, mask_in, queries_in, out,
    rows_in, whole, rows_out, coef, mask, queries, c_sem, d_sem, o_sem, i_sem,
):
    rows, _, width = conv.shape
    last = out.shape[0] - 1
    times = width // LANES
    small = [(coef_in, coef), (mask_in, mask), (queries_in, queries)]
    for k, (src, dst) in enumerate(small):
        pltpu.make_async_copy(src, dst, i_sem.at[k]).start()
    for r in range(rows):
        pltpu.make_async_copy(conv.at[r], rows_in.at[r], c_sem.at[r]).start()
    for n in range(last):
        pltpu.make_async_copy(done.at[n], whole.at[n], d_sem.at[0, n]).start()
    for k, (src, dst) in enumerate(small):
        pltpu.make_async_copy(src, dst, i_sem.at[k]).wait()
    for r in range(rows):
        pltpu.make_async_copy(conv.at[r], rows_in.at[r], c_sem.at[r]).wait()
        rows_out[r] = log_softmax_row(
            rows_in[r], across(coef[1], times), across(coef[2], times),
            mask[...], across(coef[0], times), queries[...])
        pltpu.make_async_copy(rows_out.at[r], out.at[last, :, r], o_sem.at[r]).start()
        if r == 0:
            for n in range(last):
                pltpu.make_async_copy(done.at[n], whole.at[n], d_sem.at[0, n]).wait()
                pltpu.make_async_copy(whole.at[n], out.at[n], d_sem.at[1, n]).start()
    for n in range(last):
        pltpu.make_async_copy(whole.at[n], out.at[n], d_sem.at[1, n]).wait()
    for r in range(rows):
        pltpu.make_async_copy(rows_out.at[r], out.at[last, :, r], o_sem.at[r]).wait()


def banded(
    bands, chans,
    fine, coarse, lat_weight, lat_gain, lat_shift, out_weight, out_gain, out_shift,
    mask_weight, mask_bias, queries,
):
    images, in_ch, band_rows, width = fine.shape
    share = lat_weight.shape[0]
    c_ch, c_band = coarse.shape[1], coarse.shape[2]
    rows, c_rows = band_rows // chans, c_band // chans
    query_count = queries.shape[0]
    pixel_count = float(D // GROUPS * band_rows * bands * width)
    params = [v.reshape(1, share) for v in (lat_gain, lat_shift, out_gain, out_shift, mask_bias)]
    anywhere = pl.BlockSpec(memory_space=pl.ANY)
    vmem = pl.BlockSpec(memory_space=pltpu.VMEM)
    dma = pltpu.SemaphoreType.DMA
    before = max(images - 1, 1)
    pitch = band_rows + 1 - band_rows % 2
    c_pitch = c_band
    done, conv, coef, mask = pl.pallas_call(
        functools.partial(kernel, bands, chans, pixel_count),
        out_shape=[
            jax.ShapeDtypeStruct((before, query_count, rows, width), F32),
            jax.ShapeDtypeStruct((rows, D, width), F32),
            jax.ShapeDtypeStruct((3, D, LANES), F32),
            jax.ShapeDtypeStruct((D, D), BF16),
        ],
        in_specs=[anywhere] * 10 + [vmem],
        out_specs=[anywhere] * 4,
        scratch_shapes=[
            pltpu.VMEM((images, in_ch, band_rows, width), BF16),
            pltpu.VMEM((images, c_ch, c_band, width // 2), BF16),
            pltpu.VMEM((in_ch * pitch, LANES), F32),
            pltpu.VMEM((c_ch * c_pitch, LANES), F32),
            pltpu.VMEM((images, band_rows, in_ch, width), BF16),
            pltpu.VMEM((images, c_band, c_ch, width // 2), BF16),
            pltpu.VMEM((images, rows + 2, chans * in_ch, width), BF16),
            pltpu.VMEM((images, c_rows + 2, chans * c_ch, width // 2), BF16),
            pltpu.VMEM((chans, chans * in_ch, share), BF16),
            pltpu.VMEM((5, chans, 1, share), BF16),
            pltpu.VMEM((9, D, D), BF16),
            pltpu.VMEM((1, D, D), BF16),
            pltpu.VMEM((D, chans * in_ch), BF16),
            pltpu.VMEM((D, 9 * D), BF16),
            pltpu.VMEM((images, rows + 2, D, width), F32),
            pltpu.VMEM((c_rows + 2, D, width), F32),
            pltpu.VMEM(((rows + 2) * 3 * D, width), BF16),
            pltpu.VMEM((images, rows, D, width), F32),
            pltpu.VMEM((before, rows, query_count, width), F32),
            pltpu.VMEM((2 * images, 5, D, LANES), F32),
            pltpu.VMEM((bands * chans, 1, LANES), F32),
            pltpu.VMEM((images, bands * chans, 1, LANES), F32),
            dma((2, images)),
            dma((images, chans)), dma((images, chans)),
            dma((images, 2, chans)), dma((images, 2, chans)),
            dma((images, chans)), dma((images, chans)),
            dma((images, 2, chans)), dma((images, 2, chans)),
            dma((6, chans)), dma((6, chans)), dma((2, chans)), dma((2, chans)),
            dma((2, chans, 4)), dma((2, chans, 4)),
            dma((1 + images,)), dma((1 + images,)),
            dma((before, rows)), dma((rows + 2,)),
        ],
        compiler_params=pltpu.CompilerParams(
            has_side_effects=True, collective_id=0, vmem_limit_bytes=60 * 1024 * 1024),
    )(
        fine, coarse, lat_weight.T, *params, out_weight.reshape(9, share, D), mask_weight[None],
        queries,
    )
    return pl.pallas_call(
        tail,
        out_shape=jax.ShapeDtypeStruct((images, query_count, rows, width), F32),
        in_specs=[anywhere] * 5,
        out_specs=anywhere,
        scratch_shapes=[
            pltpu.VMEM((rows, D, width), F32),
            pltpu.VMEM((before, query_count, rows, width), F32),
            pltpu.VMEM((rows, query_count, width), F32),
            pltpu.VMEM((3, D, LANES), F32),
            pltpu.VMEM((D, D), BF16),
            pltpu.VMEM((query_count, D), BF16),
            dma((rows,)), dma((2, before)), dma((rows,)), dma((3,)),
        ],
        compiler_params=pltpu.CompilerParams(vmem_limit_bytes=60 * 1024 * 1024),
    )(done, conv, coef, mask, queries)


def gathered(
    bands, chans,
    fine, coarse, lat_weight, lat_gain, lat_shift, out_weight, out_gain, out_shift,
    mask_weight, mask_bias, queries,
):
    def whole(x, axis):
        return lax.all_gather(x, "chan", axis=axis, tiled=True)

    fine, coarse = whole(fine, 1), whole(coarse, 1)
    lat_weight, mask_weight = whole(lat_weight, 0), whole(mask_weight, 0)
    out_weight = whole(out_weight, 2)
    lat_gain, lat_shift, out_gain, out_shift, mask_bias = (
        whole(v, 0).astype(F32)[None, :, None, None]
        for v in (lat_gain, lat_shift, out_gain, out_shift, mask_bias))
    images, _, band_rows, width = fine.shape
    c_band, half_w = coarse.shape[2], coarse.shape[3]
    rows = band_rows // chans
    b = lax.axis_index("band")
    count = float(D // GROUPS * band_rows * bands * width)

    def norm(x, gain, shift, over):
        grouped = x.reshape(images, GROUPS, -1)
        mean = lax.psum(jnp.sum(grouped, axis=2), over) / count
        off = grouped - mean[:, :, None]
        var = lax.psum(jnp.sum(off * off, axis=2), over) / count
        y = (off * lax.rsqrt(var + EPS)[:, :, None]).reshape(x.shape)
        return y * gain + shift

    def with_border(x, clamp):
        n = x.shape[2]
        down = [(k, (k + 1) % bands) for k in range(bands)]
        upward = [((k + 1) % bands, k) for k in range(bands)]
        above = lax.ppermute(x[:, :, n - 1:], "band", down)
        below = lax.ppermute(x[:, :, :1], "band", upward)
        above = jnp.where(b == 0, x[:, :, :1] if clamp else jnp.zeros_like(above), above)
        below = jnp.where(
            b == bands - 1, x[:, :, n - 1:] if clamp else jnp.zeros_like(below), below)
        return jnp.concatenate([above, x, below], axis=2)

    def doubled(x, axis):
        n = x.shape[axis] - 2
        low, mid, high = (lax.slice_in_dim(x, k, k + n, axis=axis) for k in range(3))
        pair = jnp.stack([0.25 * low + 0.75 * mid, 0.75 * mid + 0.25 * high], axis + 1)
        return pair.reshape(x.shape[:axis] + (2 * n,) + x.shape[axis + 1:])

    def mix(w, x):
        return jnp.einsum("oi,nirc->norc", w, x, preferred_element_type=F32)

    lateral = norm(mix(lat_weight, fine), lat_gain, lat_shift, "band")
    tall = doubled(with_border(coarse, True).astype(F32), 2)
    upsampled = doubled(jnp.pad(tall, ((0, 0), (0, 0), (0, 0), (1, 1)), mode="edge"), 3)
    joined = (lateral + upsampled).astype(BF16)
    padded = lax.dynamic_slice_in_dim(
        with_border(joined, False), lax.axis_index("chan") * rows, rows + 2, axis=2)
    padded = jnp.pad(padded, ((0, 0), (0, 0), (0, 0), (1, 1)))
    conv = sum(
        mix(out_weight[a, t], padded[:, :, a:a + rows, t:t + width])
        for a in range(3) for t in range(3))
    act = jnp.maximum(norm(conv, out_gain, out_shift, ("band", "chan")), 0.0).astype(BF16)
    features = (mix(mask_weight, act) + mask_bias).astype(BF16)
    logits = mix(queries, features)
    shifted = logits - jnp.max(logits, axis=1, keepdims=True)
    return shifted - jnp.log(jnp.sum(jnp.exp(shifted), axis=1, keepdims=True))


def per_device(bands, chans, fine, coarse, *rest):
    thick = coarse.shape[2] % chans == 0 and fine.shape[2] == 2 * coarse.shape[2]
    return (banded if thick else gathered)(bands, chans, fine, coarse, *rest)


def solution(mesh):
    return jax.shard_map(
        functools.partial(per_device, mesh.shape["band"], mesh.shape["chan"]),
        mesh=mesh,
        in_specs=(
            P(None, "chan", "band", None),
            P(None, "chan", "band", None),
            P("chan", None),
            P("chan"),
            P("chan"),
            P(None, None, "chan", None),
            P("chan"),
            P("chan"),
            P("chan", None),
            P("chan"),
            P(),
        ),
        out_specs=P(None, None, ("band", "chan"), None),
        check_vma=False,
    )
```

time: 86.9 us -> 78.5 us (0.903)
  local copies, waits for them, and re-layouts: 12 us -> 0 us
  Pallas kernels: 74.6 us -> 78.3 us
    transpose x1 -> x0, local copies, waits for them, and re-layouts: 5.74 us -> none  [per_device(): return jnp.transpose(result, (0, 2, 1, 3))]
    unnamed x2 -> x0, local copies, waits for them, and re-layouts: 4.94 us -> none
    pallas_call x1 -> x2, Pallas kernels: 74.6 us -> 78.3 us  [the longest x1 73.4 us: banded(): pl.pallas_call(functools.partial(kernel, bands, chans, pixel_count), out_...]
where the time goes in v1:
time: 78.5 us; the launch traced here: 78.3 us
  Pallas kernels  78.3 us (100%)
    pallas_call x1, Pallas kernels, banded(): pl.pallas_call(functools.partial(kernel, bands, chans, pixel_count), out_...  73.4 us
    pallas_call x1, Pallas kernels, banded(): pl.pallas_call(tail, out_shape=jax.ShapeDtypeStruct((images, query_count,...  4.87 us

profile of v1, /device:TPU:0, one launch (start us, length us, event | category | flops | bytes accessed | tf_op | source)
XLA Modules:
  0.0 78.3 jit_solution(9083760824692046010)
XLA Ops:
  0.0 73.4 %shard_map.109 = (f32[1,200,4,512]{3,2,1,0:T(4,128)}, f32[4,256,512]{2,1,0:T(8,128)}, f32[3,256,128]{2,1,0:T(8,128)}, bf16[256,256]{1,0:T(8,128)(2,1)}) custom-call(bf16[2,96,8,512]{3,2,1,0:T(8,128)(2,1)} %fine.1, bf16[2,128,4,256]{3,2,1,0:T(4,128)(2,1)} %coarse.1, bf16[192,128]{1,0:T(8,128)(2,1)} %bitcast.10, bf16[1,128]{1,0:T(2,128)(2,1)} %bitcast.11, ...), custom_call_target="tpu_custom_call" | custom-call | tf_op jit(solution)/shard_map/pallas_call | solution.py:514
  73.4 4.9 %shard_map.110 = f32[2,200,4,512]{3,2,1,0:T(4,128)} custom-call(f32[1,200,4,512]{3,2,1,0:T(4,128)} %get-tuple-element.9.done, f32[4,256,512]{2,1,0:T(8,128)} %get-tuple-element.10.conv, f32[3,256,128]{2,1,0:T(8,128)} %get-tuple-element.11.coef_in, bf16[256,256]{1,0:T(8,128)(2,1)} %get-tuple-element.12.mask_in, bf16[200,256]{1,0:T(8,128)(2,1)} %queries_in.1), custom_call_target="tpu_custom_call" | custom-call | tf_op jit(solution)/shard_map/pallas_call | solution.py:563

commit v2 on v1

--- a/solution.py
+++ b/solution.py
@@ -39,7 +39,7 @@
     bands, chans, pixel_count,
     fine, coarse, lat_in, par0, par1, par2, par3, par4, conv_in, mask_in, queries,
     done, last_conv, last_coef, mask_out,
-    raw, craw, tmp, ctmp, fsend, csend,
+    raw, craw, tmp, ctmp, fsend, csend, up,
     feats, level, ebuf, pbuf, wbuf, mbuf, wlat, wide, lat, cols_up, stacked, conv, rows_out,
     coef, stat1, stat2,
     r_sem, f_send, f_recv, fh_send, fh_recv, c_send, c_recv, ch_send, ch_recv,
@@ -133,7 +133,7 @@
                 ssem.at[n, s], rsem.at[n, s], b, t,
             )
 
-    def halo_rows(src, dst, n, size, ch, ssem, rsem):
+    def top_rows(src, dst, n, size, ch, ssem, rsem):
         for s in range(chans):
             t = lax.rem(c + s, chans)
             k = (s + 1) % chans
@@ -143,6 +143,10 @@
                 ssem.at[n, 0, s], rsem.at[n, 0, k], to // chans, lax.rem(to, chans),
                 c == 0 if k == 0 else None,
             )
+
+    def bottom_rows(src, dst, n, size, ch, ssem, rsem):
+        for s in range(chans):
+            t = lax.rem(c + s, chans)
             k = (s - 1) % chans
             to = lax.rem(b * chans + t - 1 + total, total)
             send(
@@ -168,8 +172,8 @@
         for s in range(1, chans):
             wait_on(dst.at[n, pl.ds(1, size), pl.ds(0, ch)], rsem.at[n, s])
 
-    def wait_halo(dst, n, size, ch, rsem):
-        for side in range(2):
+    def wait_halo(dst, n, size, ch, rsem, sides):
+        for side in sides:
             for s in range(chans):
                 def arrive():
                     wait_on(dst.at[n, side * (size + 1), pl.ds(0, ch)], rsem.at[n, side, s])
@@ -200,24 +204,18 @@
         pltpu.make_async_copy(coarse.at[n], craw.at[n], r_sem.at[1, n]).wait()
         by_rows(craw, csend, ctmp, n, ctmp.shape[0] // c_ch)
 
-    fine_rows(0)
     pl.semaphore_wait(barrier, total - 1)
     gather(lat_in, ebuf, e_send.at[0], e_recv.at[0])
     for k, par in enumerate((par0, par1, par2, par3, par4)):
         gather(par, pbuf.at[k], e_send.at[k + 1], e_recv.at[k + 1])
-    for n in range(images):
-        if n > 0:
-            fine_rows(n)
-        main_rows(fsend, feats, n, rows, in_ch, f_send, f_recv)
     weights_across(conv_in, wbuf, w_send.at[0], w_recv.at[0])
     for n in range(images):
+        fine_rows(n)
+        main_rows(fsend, feats, n, rows, in_ch, f_send, f_recv)
+    top_rows(fsend, feats, 0, rows, in_ch, fh_send, fh_recv)
+    bottom_rows(fsend, feats, 0, rows, in_ch, fh_send, fh_recv)
+    for n in range(images):
         coarse_rows(n)
-        halo_rows(fsend, feats, n, rows, in_ch, fh_send, fh_recv)
-        main_rows(csend, level, n, c_rows, c_ch, c_send, c_recv)
-        halo_rows(csend, level, n, c_rows, c_ch, ch_send, ch_recv)
-        if n == 0:
-            weights_across(mask_in, mbuf, w_send.at[1], w_recv.at[1])
-    for n in range(images):
         keep_own(fsend, feats, n, rows, in_ch)
         keep_own(csend, level, n, c_rows, c_ch)
 
@@ -298,6 +296,13 @@
     for s in range(chans):
         wlat[s * share:(s + 1) * share, :] = ebuf[s].astype(F32).T.astype(BF16)
 
+    src_col = lax.broadcasted_iota(jnp.int32, (half_w, width), 0)
+    dst_col = lax.broadcasted_iota(jnp.int32, (half_w, width), 1)
+    half = dst_col // 2
+    near = jnp.where(src_col == half, 0.75, 0.0)
+    other = jnp.clip(jnp.where(dst_col - 2 * half == 0, half - 1, half + 1), 0, half_w - 1)
+    up[...] = (near + jnp.where(src_col == other, 0.25, 0.0)).astype(BF16)
+
     def lateral(features):
         return jnp.dot(wlat[...], features, preferred_element_type=F32)
 
@@ -334,86 +339,80 @@
         lax.fori_loop(1, rows, step, 0)
         row1 = row1 + stat_rows(coef[n, S1], coef[n, S2], coef[n, SHIFT], n, images)
     exchange(row1, stat1, 0)
+    for n in range(images):
+        main_rows(csend, level, n, c_rows, c_ch, c_send, c_recv)
+        top_rows(csend, level, n, c_rows, c_ch, ch_send, ch_recv)
+        bottom_rows(csend, level, n, c_rows, c_ch, ch_send, ch_recv)
+        if n == 0:
+            weights_across(mask_in, mbuf, w_send.at[1], w_recv.at[1])
+        else:
+            top_rows(fsend, feats, n, rows, in_ch, fh_send, fh_recv)
+            bottom_rows(fsend, feats, n, rows, in_ch, fh_send, fh_recv)
     weights_around(wbuf, w_recv.at[0], q_send.at[0], q_recv.at[0])
 
-    src_col = lax.broadcasted_iota(jnp.int32, (half_w, width), 0)
-    dst_col = lax.broadcasted_iota(jnp.int32, (half_w, width), 1)
-    half = dst_col // 2
-    near = jnp.where(src_col == half, 0.75, 0.0)
-    other = jnp.clip(jnp.where(dst_col - 2 * half == 0, half - 1, half + 1), 0, half_w - 1)
-    up = (near + jnp.where(src_col == other, 0.25, 0.0)).astype(BF16)
-    lane_w = lax.broadcasted_iota(jnp.int32, (D, width), 1)
+    edge = lax.broadcasted_iota(jnp.int32, (D, LANES), 1)
+
+    def join(n, j, centred):
+        k = j // 2
+        w0, w1 = ((0.75, 0.25), (0.25, 0.75))[j % 2]
+        upsampled = w0 * cols_up[k] + w1 * cols_up[k + 1]
+        joined = (
+            centred * across(coef[n, SCALE], times) + across(coef[n, OFFSET], times) + upsampled)
+        if j == 0:
+            joined = jnp.where(me > 0, joined, 0.0)
+        if j == rows + 1:
+            joined = jnp.where(me < total - 1, joined, 0.0)
+        left = pltpu.roll(joined, 1, 1)
+        right = pltpu.roll(joined, width - 1, 1)
+        first = jnp.where(edge == 0, 0.0, left[:, :LANES])
+        final = jnp.where(edge == LANES - 1, 0.0, right[:, width - LANES:])
+        left = jnp.concatenate([first, left[:, LANES:]], axis=1)
+        right = jnp.concatenate([right[:, :width - LANES], final], axis=1)
+        base = j * 3 * D
+        stacked[base:base + D] = left.astype(BF16)
+        stacked[base + D:base + 2 * D] = joined.astype(BF16)
+        stacked[base + 2 * D:base + 3 * D] = right.astype(BF16)
 
     for n in range(images):
-        wait_halo(feats, n, rows, in_ch, fh_recv)
-        for j in (0, rows + 1):
-            lat[n, j] = lateral(feats[n, j]) - across(coef[n, SHIFT], times)
+        slot = images + n
+        wait_main(level, n, c_rows, c_ch, c_recv)
+        wait_halo(level, n, c_rows, c_ch, ch_recv, (0, 1))
+        for k in range(c_rows + 2):
+            cols_up[k] = jnp.dot(level[n, k], up[...], preferred_element_type=F32)
+
+        @pl.when(me == 0)
+        def _():
+            cols_up[0] = cols_up[1]
+
+        @pl.when(me == total - 1)
+        def _():
+            cols_up[c_rows + 1] = cols_up[c_rows]
+
         if n == 0:
             norms = combined(stat1, 0, images)
             for m in range(images):
                 set_norm(m, norms[m][0], norms[m][1], lat_gain, lat_shift)
-        wait_main(level, n, c_rows, c_ch, c_recv)
-        wait_halo(level, n, c_rows, c_ch, ch_recv)
-
-        def widen(k, carry, n=n):
-            cols_up[k] = jnp.dot(level[n, k], up, preferred_element_type=F32)
-            return carry
-
-        lax.fori_loop(0, c_rows + 2, widen, 0)
-
-        @pl.when(me == 0)
-        def _():
-            cols_up[0] = cols_up[1]
-
-        @pl.when(me == total - 1)
-        def _():
-            cols_up[c_rows + 1] = cols_up[c_rows]
-
-        def join(j, carry, n=n):
-            k = j // 2
-            even = j - 2 * k == 0
-            w0 = jnp.where(even, 0.75, 0.25)
-            w1 = jnp.where(even, 0.25, 0.75)
-            upsampled = w0 * cols_up[k] + w1 * cols_up[k + 1]
-            joined = (
-                lat[n, j] * across(coef[n, SCALE], times)
-                + across(coef[n, OFFSET], times) + upsampled)
-            inside = jnp.logical_and(me * rows + j >= 1, me * rows + j <= total * rows)
-            joined = jnp.where(inside, joined, 0.0)
-            left = jnp.where(lane_w == 0, 0.0, pltpu.roll(joined, 1, 1))
-            right = jnp.where(lane_w == width - 1, 0.0, pltpu.roll(joined, width - 1, 1))
-            base = pl.multiple_of(j * 3 * D, D)
-            stacked[pl.ds(base, D)] = left.astype(BF16)
-            stacked[pl.ds(base + D, D)] = joined.astype(BF16)
-            stacked[pl.ds(base + 2 * D, D)] = right.astype(BF16)
-            return carry
-
-        lax.fori_loop(0, rows + 2, join, 0)
-        if n == 0:
             wait_weights(wbuf, w_recv.at[0], q_recv.at[0])
             for k in range(9):
                 wide[:, k * D:(k + 1) * D] = wbuf[k]
 
-        def convolve(r):
-            base = pl.multiple_of(r * 3 * D, D)
-            return jnp.dot(wide[...], stacked[pl.ds(base, 9 * D)], preferred_element_type=F32)
-
-        slot = images + n
-
-        def keep(r, y, n=n, slot=slot):
+        def convolve(r, first=False, n=n, slot=slot):
+            y = jnp.dot(
+                wide[...], stacked[r * 3 * D:(r + 3) * 3 * D], preferred_element_type=F32)
+            if first:
+                centre_first(y, slot)
             conv[n, r] = centre(y, slot)
             if n == last:
                 pltpu.make_async_copy(conv.at[n, r], last_conv.at[r], k_sem.at[r]).start()
 
-        y = convolve(0)
-        centre_first(y, slot)
-        keep(0, y)
-
-        def more(r, carry):
-            keep(r, convolve(r))
-            return carry
-
-        lax.fori_loop(1, rows, more, 0)
+        for j in range(1, rows + 1):
+            join(n, j, lat[n, j])
+        for r in range(1, rows - 1):
+            convolve(r, r == 1)
+        for side, j, r in ((0, 0, 0), (1, rows + 1, rows - 1)):
+            wait_halo(feats, n, rows, in_ch, fh_recv, (side,))
+            join(n, j, lateral(feats[n, j]) - across(coef[n, SHIFT], times))
+            convolve(r, r == 0 and rows == 2)
         exchange(
             stat_rows(coef[slot, S1], coef[slot, S2], coef[slot, SHIFT], 0, 1), stat2.at[n], 1 + n)
         if n == 0:
@@ -528,6 +527,7 @@
             pltpu.VMEM((c_ch * c_pitch, LANES), F32),
             pltpu.VMEM((images, band_rows, in_ch, width), BF16),
             pltpu.VMEM((images, c_band, c_ch, width // 2), BF16),
+            pltpu.VMEM((width // 2, width), BF16),
             pltpu.VMEM((images, rows + 2, chans * in_ch, width), BF16),
             pltpu.VMEM((images, c_rows + 2, chans * c_ch, width // 2), BF16),
             pltpu.VMEM((chans, chans * in_ch, share), BF16),

time: 78.5 us -> 66.7 us (0.85)
  Pallas kernels: 78.3 us -> 66.3 us
    pallas_call x1, Pallas kernels: 73.4 us -> 61.5 us  [banded(): pl.pallas_call(functools.partial(kernel, bands, chans, pixel_count), out_...]
where the time goes in v2:
time: 66.7 us; the launch traced here: 66.5 us
  Pallas kernels  66.3 us (99%)
    pallas_call x1, Pallas kernels, banded(): pl.pallas_call(functools.partial(kernel, bands, chans, pixel_count), out_...  61.5 us
    pallas_call x1, Pallas kernels, banded(): pl.pallas_call(tail, out_shape=jax.ShapeDtypeStruct((images, query_count,...  4.87 us

profile of v2, /device:TPU:0, one launch (start us, length us, event | category | flops | bytes accessed | tf_op | source)
XLA Modules:
  0.0 66.5 jit_solution(12969106646046353487)
XLA Ops:
  0.0 61.5 %shard_map.109 = (f32[1,200,4,512]{3,2,1,0:T(4,128)}, f32[4,256,512]{2,1,0:T(8,128)}, f32[3,256,128]{2,1,0:T(8,128)}, bf16[256,256]{1,0:T(8,128)(2,1)}) custom-call(bf16[2,96,8,512]{3,2,1,0:T(8,128)(2,1)} %fine.1, bf16[2,128,4,256]{3,2,1,0:T(4,128)(2,1)} %coarse.1, bf16[192,128]{1,0:T(8,128)(2,1)} %bitcast.10, bf16[1,128]{1,0:T(2,128)(2,1)} %bitcast.11, ...), custom_call_target="tpu_custom_call" | custom-call | tf_op jit(solution)/shard_map/pallas_call | solution.py:513
  61.5 4.9 %shard_map.110 = f32[2,200,4,512]{3,2,1,0:T(4,128)} custom-call(f32[1,200,4,512]{3,2,1,0:T(4,128)} %get-tuple-element.9.done, f32[4,256,512]{2,1,0:T(8,128)} %get-tuple-element.10.conv, f32[3,256,128]{2,1,0:T(8,128)} %get-tuple-element.11.coef_in, bf16[256,256]{1,0:T(8,128)(2,1)} %get-tuple-element.12.mask_in, bf16[200,256]{1,0:T(8,128)(2,1)} %queries_in.1), custom_call_target="tpu_custom_call" | custom-call | tf_op jit(solution)/shard_map/pallas_call | solution.py:563
